TPU v7x, 128 devices: a whole 4x4x4 slice. The times are simulated.
128 devices in a mesh: rep: 8 (over z, y_lo), fsdp: 16 (over y_hi, x, core).
Axes of the slice: x: 4, y: 4 (y_hi: 2, y_lo: 2; y = y_hi * 2 + y_lo), z: 4, core: 2. Of those that a mesh axis runs over, the one named last changes fastest.
Arguments:
- tokens: bfloat16 [65536, 2048], P(('rep', 'fsdp')), may hold values from -6 to 6
- norm_gain: float32 [2048], replicated, may hold values from 0.5 to 1.5
- outer_params: float32 [2, 2048, 4096], P(None, 'fsdp'), may hold values from -6 to 6
- momentum: float32 [2, 2048, 4096], P(None, 'fsdp'), may hold values from -6 to 6
- deltas: bfloat16 [8, 2, 2048, 4096], P('rep', None, 'fsdp'), may hold values from -6 to 6
Outputs:
- new_params: float32 [2, 2048, 4096], P(None, 'fsdp')
- new_momentum: float32 [2, 2048, 4096], P(None, 'fsdp')
- hidden: bfloat16 [65536, 4096], P(('rep', 'fsdp'))
All inputs are finite; a program needn't handle non-finite values.
Results may differ from a plain program's by a relative error of at most 0.01.
Values may be sent and summed in bfloat16 or wider, within the bound.
A program may use at most 192 MiB of HBM per device.

v0:
```python
import math

import jax
import jax.numpy as jnp
from jax import lax
from jax.sharding import PartitionSpec as P

EPS = 1e-05
MU = 0.9
RATE = 0.7


def advance(params, moment, summed, groups):
    outer_grad = summed * (1.0 / groups)
    moment_next = MU * moment + outer_grad
    params_next = params - RATE * (outer_grad + MU * moment_next)
    return (params_next, moment_next)


def body(tokens, norm_gain, outer_params, momentum, deltas):
    groups = lax.axis_size("rep")
    own_delta = deltas[0].astype(jnp.float32)
    summed = lax.psum(own_delta.astype(jnp.bfloat16), "rep").astype(jnp.float32)
    new_params, new_momentum = advance(outer_params, momentum, summed, groups)
    weights = new_params.astype(jnp.bfloat16)
    values = tokens.astype(jnp.float32)
    scale_rows = lax.rsqrt(jnp.mean(values * values, axis=-1, keepdims=True) + EPS)
    normed = (values * scale_rows * norm_gain).astype(jnp.bfloat16)
    factor = 1.0 / math.sqrt(normed.shape[1])
    results = []
    for which in range(2):
        results.append(
            jnp.dot(
                normed,
                lax.all_gather(weights[which], "fsdp", axis=0, tiled=True),
                preferred_element_type=jnp.float32,
            )
        )
    gate, up = (results[0], results[1])
    hidden = (jax.nn.silu(gate * factor) * (up * factor)).astype(jnp.bfloat16)
    return (new_params, new_momentum, hidden)


def solution(mesh):
    in_specs = (
        P(("rep", "fsdp"), None),
        P(),
        P(None, "fsdp", None),
        P(None, "fsdp", None),
        P("rep", None, "fsdp", None),
    )
    out_specs = (P(None, "fsdp", None), P(None, "fsdp", None), P(("rep", "fsdp"), None))
    return jax.shard_map(body, mesh=mesh, in_specs=in_specs, out_specs=out_specs, check_vma=False)
```

profile of v0, /device:TPU:1, one launch (start us, length us, event | category | flops | bytes accessed | tf_op | source)
XLA Modules:
  0.0 376.3 jit_solution(11234318730406531627)
XLA Ops:
  7.2 0.0 all-reduce.2.cloned.1.call-start
  7.2 0.7 all-reduce.2.cloned.1.call-update
  7.9 0.0 all-gather.7.cloned.1.call-start
  7.9 109.9 %all-reduce.2.cloned.1.call-done = bf16[2,128,4096]{2,1,0:T(8,128)(2,1)} async-done(((bf16[2,128,4096]{2,1,0:T(8,128)(2,1)}), bf16[2,128,4096]{2,1,0:T(8,128)(2,1)}) %all-reduce.2.cloned.1.call-update) | async-done | bytes 2097168 | tf_op jit(solution)/shard_map/psum | solution.py:23
  117.9 9.4 %fusion.11 = (bf16[2,128,4096]{2,1,0:T(8,128)(2,1)S(1)}, f32[2,128,4096]{2,1,0:T(8,128)}, f32[2,128,4096]{2,1,0:T(8,128)}) fusion(f32[2,128,4096]{2,1,0:T(8,128)} %param.7, bf16[2,128,4096]{2,1,0:T(8,128)(2,1)} %all-reduce.2.cloned.1.call-done, f32[2,128,4096]{2,1,0:T(8,128)} %param.8), kind=kLoop, calls=%fused_computation.14 | loop fusion | flops 9437184 | bytes 20971520 | tf_op jit(solution)/shard_map/convert_element_type | solution.py:25
  127.3 0.0 copy-start
  127.3 0.0 copy-start.1
  127.3 1.5 fusion.12
  128.7 0.0 all-gather.7.cloned.1.call-update
  128.7 0.0 all-gather.5.cloned.1.call-start
  128.8 0.7 all-gather.5.cloned.1.call-update
  129.5 0.1 copy-done
  129.6 0.5 fusion.6
  130.1 108.7 %all-gather.7.cloned.1.call-done = bf16[1,2048,4096]{2,1,0:T(8,128)(2,1)} async-done(((bf16[1,128,4096]{2,1,0:T(8,128)(2,1)}), bf16[1,2048,4096]{2,1,0:T(8,128)(2,1)}) %all-gather.7.cloned.1.call-update) | async-done | bytes 16777232 | tf_op jit(solution)/shard_map/all_gather | solution.py:35
  238.8 0.0 copy-done.1
  238.8 14.4 %fusion = f32[512,4096]{1,0:T(8,128)} fusion(bf16[1,2048,4096]{2,1,0:T(8,128)(2,1)} %all-gather.7.cloned.1.call-done, bf16[512,2048]{1,0:T(8,128)(2,1)S(1)} %copy-done, f32[2048]{0:T(1024)S(1)} %copy-done.1, f32[512]{0:T(512)S(1)} %add_rsqrt_fusion), kind=kOutput, calls=%fused_computation | convolution fusion | flops 8594128896 | bytes 27273216 | tf_op jit(solution)/shard_map/dot_general | solution.py:33
  253.2 96.1 %all-gather.5.cloned.1.call-done = bf16[1,2048,4096]{2,1,0:T(8,128)(2,1)} async-done(((bf16[1,128,4096]{2,1,0:T(8,128)(2,1)}), bf16[1,2048,4096]{2,1,0:T(8,128)(2,1)}) %all-gather.5.cloned.1.call-update) | async-done | bytes 16777232 | tf_op jit(solution)/shard_map/all_gather | solution.py:35
  349.3 20.5 %multiply_convert_fusion = bf16[512,4096]{1,0:T(8,128)(2,1)} fusion(f32[512,4096]{1,0:T(8,128)} %fusion, bf16[1,2048,4096]{2,1,0:T(8,128)(2,1)} %all-gather.5.cloned.1.call-done, bf16[512,2048]{1,0:T(8,128)(2,1)S(1)} %copy-done, f32[2048]{0:T(1024)S(1)} %copy-done.1, f32[512]{0:T(512)S(1)} %add_rsqrt_fusion), kind=kOutput, calls=%fused_computation.4 | convolution fusion | flops 8610906112 | bytes 31467520 | tf_op jit(solution)/shard_map/dot_general | solution.py:33
  (1 shorter events, 0.0 us)
Async XLA Ops:
  7.2 110.7 %all-reduce.2.cloned.1.call-start = ((), (), s32[]{:S(2)}) async-start(), calls=%async_computation | async-start | bytes 4194304 | tf_op jit(solution)/shard_map/psum | solution.py:23
  7.9 230.9 %all-gather.7.cloned.1.call-start = ((), (), s32[]{:S(2)}) async-start(), calls=%async_computation.2 | async-start | bytes 17825792 | tf_op jit(solution)/shard_map/all_gather | solution.py:35
  127.3 2.3 copy-start
  127.3 111.6 %copy-start.1 = (f32[2048]{0:T(1024)S(1)}, f32[2048]{0:T(1024)}, u32[]{:S(2)}) copy-start(f32[2048]{0:T(1024)} %param.6) | copy-start | bytes 24580
  128.7 220.6 %all-gather.5.cloned.1.call-start = ((), (), s32[]{:S(2)}) async-start(), calls=%async_computation.1 | async-start | bytes 17825792 | tf_op jit(solution)/shard_map/all_gather | solution.py:35
Sparse Core Ops, SparseCore 0:
  10.5 107.3 all-reduce.1
  128.9 109.9 all-gather.6
  241.8 107.4 all-gather.4
where the time goes:
time: 376 us
  waiting for transfers between devices  316 us (84%)
  matrix products  34.9 us (9%)
  between operations  13.7 us (4%)
  other arithmetic  9.89 us (3%)
    all_gather x2, waiting for transfers between devices, body(): lax.all_gather(weights[which], 'fsdp', axis=0, tiled=True)  205 us
    psum x1, waiting for transfers between devices, body(): summed = lax.psum(own_delta.astype(jnp.bfloat16), 'rep').astype(jnp.float32)  110 us
    dot_general x2, matrix products, body(): jnp.dot(normed, lax.all_gather(weights[which], 'fsdp', axis=0, tiled=True...  34.9 us
    convert_element_type x1, other arithmetic, body(): weights = new_params.astype(jnp.bfloat16)  9.4 us
  transfers between devices with their start and end apart: 3, of which 3 were waited for; matrix products, arithmetic and copies ran while one was open for 4% of the time, Pallas kernels for 0%

commit v1 on v0

v1 whole, which is shorter than its diff:
```python
import functools
import math

import jax
import jax.numpy as jnp
from jax import lax
from jax.experimental import pallas as pl
from jax.experimental.pallas import tpu as pltpu
from jax.sharding import PartitionSpec as P

EPS = 1e-05
MU = 0.9
RATE = 0.7
MESH = pl.DeviceIdType.MESH

CHUNKS = 8
GROUPS = 8
XS = 4


def kernel(
    tok_ref, gain_ref, p_ref, m_ref, d_ref,
    sums_ref, hid_ref,
    dl, rs, sm, pb, mb, w, stg, tk, nt, ob,
    ld_d, ld_p, ld_m, ld_t,
    rs_s, rs_r, sm_s, sm_r, d2_s, d2_r, nt_s, nt_r,
    yo_s, yo_r, x_s, x_r, f_s, f_r, o_l, o_s, o_r, so_s,
):
    n = CHUNKS
    rows = dl.shape[3]
    wc = dl.shape[4]
    half = n * wc
    piece = rows // GROUPS
    tokens = tk.shape[0]
    width = tk.shape[1]

    rep = lax.axis_index("rep")
    fs = lax.axis_index("fsdp")
    core = lax.rem(fs, 2)
    other = 1 - core
    chip = fs // 2
    x = lax.rem(chip, XS)
    yh = chip // XS
    yl = lax.rem(rep, 2)
    z = rep // 2
    x_up = lax.rem(x + 1, XS)
    x_dn = lax.rem(x + XS - 1, XS)

    def fsdp_of(yh_, x_, core_):
        return (yh_ * XS + x_) * 2 + core_

    partner = (rep, fsdp_of(yh, x, other))
    across = (z * 2 + 1 - yl, fsdp_of(1 - yh, x, core))
    up = (rep, fsdp_of(yh, x_up, core))
    down = (rep, fsdp_of(yh, x_dn, core))
    peers = [(lax.rem(rep + k, GROUPS), fs) for k in range(1, GROUPS)]

    def load(src, dst, sem, j, h):
        return pltpu.make_async_copy(
            src.at[:, :, pl.ds(pl.multiple_of(h * half + j * wc, wc), wc)],
            dst.at[j, h],
            sem.at[j, h],
        )

    def remote(src, dst, send, recv, device):
        return pltpu.make_async_remote_copy(
            src_ref=src, dst_ref=dst, send_sem=send, recv_sem=recv,
            device_id=device, device_id_type=MESH,
        )

    def rs_copy(j, k):
        rows_of = pl.multiple_of(peers[k][0] * piece, piece)
        return remote(
            dl.at[j, :, :, pl.ds(rows_of, piece), :], rs.at[j, k],
            rs_s.at[j, k], rs_r.at[j, k], peers[k],
        )

    def sm_copy(j, k):
        mine = pl.ds(pl.multiple_of(rep * piece, piece), piece)
        ref = sm.at[j, :, :, mine, :]
        return remote(ref, ref, sm_s.at[j, k], sm_r.at[j, k], peers[k])

    def d2_copy(j):
        at = pl.ds(pl.multiple_of(core * rows, rows), rows)
        return remote(
            stg.at[j], w.at[j, :, yh, x, at, :], d2_s.at[j], d2_r.at[j], partner
        )

    def yo_copy(j):
        ref = w.at[j, :, yh, x]
        return remote(ref, ref, yo_s.at[j], yo_r.at[j], across)

    def x_copy(j, k):
        ref = w.at[j, :, :, x]
        return remote(ref, ref, x_s.at[j, k], x_r.at[j, k], (up, down)[k])

    def f_copy(j, k):
        ref = w.at[j, :, :, (x_dn, x_up)[k], pl.ds(k * rows, rows), :]
        return remote(ref, ref, f_s.at[j, k], f_r.at[j, k], (up, down)[k])

    def nt_copy():
        ref = nt.at[pl.ds(pl.multiple_of(core * tokens, tokens), tokens), :]
        return remote(ref, ref, nt_s.at[0], nt_r.at[0], partner)

    def column(j):
        return pl.ds(pl.multiple_of(core * half + j * wc, wc), wc)

    def own_out(j):
        at = pl.ds(pl.multiple_of(core * tokens, tokens), tokens)
        return pltpu.make_async_copy(
            ob.at[j, at, :], hid_ref.at[:, column(j)], o_l.at[j]
        )

    def far_out(j):
        at = pl.ds(pl.multiple_of(other * tokens, tokens), tokens)
        return remote(
            ob.at[j, at, :], hid_ref.at[:, column(j)], o_s.at[j], o_r.at[j], partner
        )

    def sums_out(j, h):
        return pltpu.make_async_copy(
            sm.at[j, h],
            sums_ref.at[:, :, pl.ds(pl.multiple_of(h * half + j * wc, wc), wc)],
            so_s.at[j, h],
        )

    def both(fn):
        for h in range(2):
            fn(h)

    @pl.loop(0, n)
    def _(j):
        both(lambda h: load(d_ref, dl, ld_d, j, h).start())

    pltpu.make_async_copy(tok_ref, tk, ld_t.at[0]).start()

    @pl.loop(0, n)
    def _(j):
        both(lambda h: load(p_ref, pb, ld_p, j, h).start())
        both(lambda h: load(m_ref, mb, ld_m, j, h).start())

    barrier = pltpu.get_barrier_semaphore()
    friends = peers + [partner, across, up, down]
    for friend in friends:
        pl.semaphore_signal(barrier, inc=1, device_id=friend, device_id_type=MESH)
    pl.semaphore_wait(barrier, len(friends))

    def scatter(j):
        both(lambda h: load(d_ref, dl, ld_d, j, h).wait())
        for k in range(GROUPS - 1):
            rs_copy(j, k).start()

    for j in range(2):
        scatter(j)

    pltpu.make_async_copy(tok_ref, tk, ld_t.at[0]).wait()
    step = 32

    @pl.loop(0, tokens // step)
    def _(i):
        at = pl.multiple_of(i * step, step)
        values = tk[pl.ds(at, step), :].astype(jnp.float32)
        mean = jnp.sum(values * values, axis=1, keepdims=True) * (1.0 / width)
        scaled = values * lax.rsqrt(mean + EPS) * gain_ref[...]
        base = pl.multiple_of(core * tokens + at, step)
        nt[pl.ds(base, step), :] = scaled.astype(jnp.bfloat16)

    def add_up(j):
        for k in range(GROUPS - 1):
            rs_copy(j, k).wait_recv()
        mine = pl.ds(pl.multiple_of(rep * piece, piece), piece)
        for h in range(2):
            for q in range(2):
                total = dl[j, h, q, mine, :].astype(jnp.float32)
                for k in range(GROUPS - 1):
                    total = total + rs[j, k, h, q].astype(jnp.float32)
                sm[j, h, q, mine, :] = total.astype(jnp.bfloat16)

    def update(j):
        for k in range(GROUPS - 1):
            sm_copy(j, k).wait_recv()
        both(lambda h: load(p_ref, pb, ld_p, j, h).wait())
        both(lambda h: load(m_ref, mb, ld_m, j, h).wait())
        at = pl.ds(pl.multiple_of(core * rows, rows), rows)

        def weights(h, q):
            grad = sm[j, h, q].astype(jnp.float32) * (1.0 / GROUPS)
            moment = MU * mb[j, h, q] + grad
            fresh = pb[j, h, q] - RATE * (grad + MU * moment)
            return fresh.astype(jnp.bfloat16)

        for q in range(2):
            stg[j, q] = weights(other, q)
        for q in range(2):
            w[j, q, yh, x, at, :] = weights(core, q)
        both(lambda h: sums_out(j, h).start())

    factor = 1.0 / math.sqrt(width)
    tile = 256

    def project(j):
        @pl.loop(0, 2 * tokens // tile)
        def _(i):
            at = pl.ds(pl.multiple_of(i * tile, tile), tile)
            left = nt[at, :]
            gate = jnp.dot(
                left, w[j, 0].reshape(width, wc), preferred_element_type=jnp.float32
            ) * factor
            raised = jnp.dot(
                left, w[j, 1].reshape(width, wc), preferred_element_type=jnp.float32
            ) * factor
            ob[j, at, :] = (gate / (1.0 + jnp.exp(-gate)) * raised).astype(jnp.bfloat16)

    nt_copy().start()

    @pl.loop(0, n + 5)
    def _(t):
        def stage(lag, fn):
            j = t - lag

            @pl.when(jnp.logical_and(j >= 0, j < n))
            def _():
                fn(j)

        def stage_x(j):
            yo_copy(j).wait_recv()
            for k in range(2):
                x_copy(j, k).start()

        def stage_y(j):
            d2_copy(j).wait_recv()
            yo_copy(j).start()

        def stage_send_sums(j):
            for k in range(GROUPS - 1):
                sm_copy(j, k).start()

        def stage_forward(j):
            for k in range(2):
                x_copy(j, k).wait_recv()
                f_copy(j, k).start()

        def stage_project(j):
            for k in range(2):
                f_copy(j, k).wait_recv()

            @pl.when(j == 0)
            def _():
                nt_copy().wait_recv()

            project(j)
            own_out(j).start()
            far_out(j).start()

        stage(3, stage_x)
        stage(2, stage_y)
        stage(1, update)
        stage(0, add_up)
        stage(1, lambda j: d2_copy(j).start())
        stage(-2, scatter)
        stage(0, stage_send_sums)
        stage(4, stage_forward)
        stage(5, stage_project)

    nt_copy().wait_send()

    @pl.loop(0, n)
    def _(j):
        for k in range(GROUPS - 1):
            rs_copy(j, k).wait_send()
            sm_copy(j, k).wait_send()
        d2_copy(j).wait_send()
        yo_copy(j).wait_send()
        for k in range(2):
            x_copy(j, k).wait_send()
            f_copy(j, k).wait_send()
        both(lambda h: sums_out(j, h).wait())
        own_out(j).wait()
        far_out(j).wait_send()
        far_out(j).wait_recv()


def fused(tokens, gain, params, moment, deltas):
    count, width = tokens.shape
    _, rows, cols = params.shape
    n = CHUNKS
    wc = cols // (2 * n)
    piece = rows // GROUPS
    bf16, f32 = jnp.bfloat16, jnp.float32
    dma = pltpu.SemaphoreType.DMA
    any_spec = pl.BlockSpec(memory_space=pl.ANY)
    return pl.pallas_call(
        kernel,
        out_shape=(
            jax.ShapeDtypeStruct((2, rows, cols), bf16),
            jax.ShapeDtypeStruct((count, cols), bf16),
        ),
        in_specs=[any_spec, pl.BlockSpec(memory_space=pltpu.VMEM), any_spec, any_spec, any_spec],
        out_specs=(any_spec, any_spec),
        scratch_shapes=[
            pltpu.VMEM((n, 2, 2, rows, wc), bf16),
            pltpu.VMEM((n, GROUPS - 1, 2, 2, piece, wc), bf16),
            pltpu.VMEM((n, 2, 2, rows, wc), bf16),
            pltpu.VMEM((n, 2, 2, rows, wc), f32),
            pltpu.VMEM((n, 2, 2, rows, wc), f32),
            pltpu.VMEM((n, 2, 2, XS, 2 * rows, wc), bf16),
            pltpu.VMEM((n, 2, rows, wc), bf16),
            pltpu.VMEM((count, width), bf16),
            pltpu.VMEM((2 * count, width), bf16),
            pltpu.VMEM((n, 2 * count, wc), bf16),
            dma((n, 2)), dma((n, 2)), dma((n, 2)), dma((1,)),
            dma((n, GROUPS - 1)), dma((n, GROUPS - 1)),
            dma((n, GROUPS - 1)), dma((n, GROUPS - 1)),
            dma((n,)), dma((n,)), dma((1,)), dma((1,)),
            dma((n,)), dma((n,)),
            dma((n, 2)), dma((n, 2)), dma((n, 2)), dma((n, 2)),
            dma((n,)), dma((n,)), dma((n,)), dma((n, 2)),
        ],
        compiler_params=pltpu.CompilerParams(
            collective_id=0, has_side_effects=True, vmem_limit_bytes=60 * 2**20
        ),
        cost_estimate=pl.CostEstimate(
            flops=4 * count * width * cols, bytes_accessed=2**25, transcendentals=count * cols
        ),
    )(tokens, gain, params, moment, deltas)


def body(tokens, norm_gain, outer_params, momentum, deltas):
    sums, hidden = fused(
        tokens, norm_gain.reshape(1, -1), outer_params, momentum, deltas[0]
    )
    outer_grad = sums.astype(jnp.float32) * (1.0 / GROUPS)
    new_momentum = MU * momentum + outer_grad
    new_params = outer_params - RATE * (outer_grad + MU * new_momentum)
    return (new_params, new_momentum, hidden)


def solution(mesh):
    in_specs = (
        P(("rep", "fsdp"), None),
        P(),
        P(None, "fsdp", None),
        P(None, "fsdp", None),
        P("rep", None, "fsdp", None),
    )
    out_specs = (P(None, "fsdp", None), P(None, "fsdp", None), P(("rep", "fsdp"), None))
    return jax.shard_map(body, mesh=mesh, in_specs=in_specs, out_specs=out_specs, check_vma=False)
```

time: 376 us -> 189 us (0.50)
  waiting for transfers between devices: 316 us -> 0 us
  Pallas kernels: 0 us -> 177 us
  matrix products: 34.9 us -> 0 us
  between operations: 13.7 us -> 0.65 us
    all_gather x2 -> x0, waiting for transfers between devices: 205 us -> none  [body(): lax.all_gather(weights[which], 'fsdp', axis=0, tiled=True)]
    pallas_call x0 -> x1, Pallas kernels: none -> 177 us  [fused(): pl.pallas_call(kernel, out_shape=(jax.ShapeDtypeStruct((2, rows, cols), b...]
    psum x1 -> x0, waiting for transfers between devices: 110 us -> none  [body(): summed = lax.psum(own_delta.astype(jnp.bfloat16), 'rep').astype(jnp.float32)]
    dot_general x2 -> x0, matrix products: 34.9 us -> none  [body(): jnp.dot(normed, lax.all_gather(weights[which], 'fsdp', axis=0, tiled=True...]
    sub x0 -> x1, other arithmetic: none -> 9.47 us  [body(): new_params = outer_params - RATE * (outer_grad + MU * new_momentum)]
    convert_element_type x1 -> x0, other arithmetic: 9.4 us -> none  [body(): weights = new_params.astype(jnp.bfloat16)]
  transfers between devices with their start and end apart: 3 -> 0, of which waited for: 3 -> 0; matrix products, arithmetic and copies ran while one was open for 4% -> 0% of each run, Pallas kernels for 0% -> 0%
where the time goes in v1:
time: 189 us
  Pallas kernels  177 us (94%)
  other arithmetic  9.47 us (5%)
  local copies, waits for them, and re-layouts  2.02 us (1%)
    pallas_call x1, Pallas kernels, fused(): pl.pallas_call(kernel, out_shape=(jax.ShapeDtypeStruct((2, rows, cols), b...  177 us
    sub x1, other arithmetic, body(): new_params = outer_params - RATE * (outer_grad + MU * new_momentum)  9.47 us

profile of v1, /device:TPU:1, one launch (start us, length us, event | category | flops | bytes accessed | tf_op | source)
XLA Modules:
  0.0 189.0 jit_solution(4899743758641997173)
XLA Ops:
  0.6 176.9 %shard_map.76 = (bf16[2,128,4096]{2,1,0:T(8,128)(2,1)}, bf16[512,4096]{1,0:T(8,128)(2,1)}) custom-call(bf16[512,2048]{1,0:T(8,128)(2,1)} %tok_ref.1, f32[1,2048]{1,0:T(1,128)} %bitcast.3, f32[2,128,4096]{2,1,0:T(8,128)} %p_ref.1, f32[2,128,4096]{2,1,0:T(8,128)} %m_ref.1, bf16[2,128,4096]{2,1,0:T(8,128)(2,1)} %bitcast.2), custom_call_target="tpu_custom_call" | custom-call | flops 17179869184 | bytes 33554432 | tf_op jit(solution)/shard_map/pallas_call | solution.py:292
  177.5 0.0 copy-start
  177.5 9.5 %multiply_subtract_fusion = (f32[2,128,4096]{2,1,0:T(8,128)}, f32[2,128,4096]{2,1,0:T(8,128)}) fusion(f32[2,128,4096]{2,1,0:T(8,128)} %p_ref.1, bf16[2,128,4096]{2,1,0:T(8,128)(2,1)} %get-tuple-element.5, f32[2,128,4096]{2,1,0:T(8,128)} %m_ref.1), kind=kLoop, calls=%fused_computation | loop fusion | flops 8388608 | bytes 18874368 | tf_op jit(solution)/shard_map/sub | solution.py:334
  187.0 0.0 copy-done
  187.0 2.0 %copy.9 = bf16[512,4096]{1,0:T(8,128)(2,1)} copy(bf16[512,4096]{1,0:T(8,128)(2,1)S(1)} %copy-done) | data formatting | bytes 8388608
Async XLA Ops:
  177.5 9.5 %copy-start = (bf16[512,4096]{1,0:T(8,128)(2,1)S(1)}, bf16[512,4096]{1,0:T(8,128)(2,1)}, u32[]{:S(2)}) copy-start(bf16[512,4096]{1,0:T(8,128)(2,1)} %get-tuple-element.14) | copy-start | bytes 12582916

commit v2 on v1

--- a/solution.py
+++ b/solution.py
@@ -16,6 +16,10 @@
 CHUNKS = 8
 GROUPS = 8
 XS = 4
+ZS = 4
+PART_X = 96
+PART_Y = 96
+PART_Z = 64
 
 
 def kernel(
@@ -24,7 +28,7 @@
     dl, rs, sm, pb, mb, w, stg, tk, nt, ob,
     ld_d, ld_p, ld_m, ld_t,
     rs_s, rs_r, sm_s, sm_r, d2_s, d2_r, nt_s, nt_r,
-    yo_s, yo_r, x_s, x_r, f_s, f_r, o_l, o_s, o_r, so_s,
+    yo_s, yo_r, x_s, x_r, f_s, f_r, yi_s, yi_r, z_s, z_r, o_l, o_s, o_r, so_s,
 ):
     n = CHUNKS
     rows = dl.shape[3]
@@ -45,6 +49,7 @@
     z = rep // 2
     x_up = lax.rem(x + 1, XS)
     x_dn = lax.rem(x + XS - 1, XS)
+    x_far = lax.rem(x + 2, XS)
 
     def fsdp_of(yh_, x_, core_):
         return (yh_ * XS + x_) * 2 + core_
@@ -53,6 +58,8 @@
     across = (z * 2 + 1 - yl, fsdp_of(1 - yh, x, core))
     up = (rep, fsdp_of(yh, x_up, core))
     down = (rep, fsdp_of(yh, x_dn, core))
+    beside = (z * 2 + 1 - yl, fs)
+    layers = [(lax.rem(z + k, ZS) * 2 + yl, fs) for k in (1, 2, 3)]
     peers = [(lax.rem(rep + k, GROUPS), fs) for k in range(1, GROUPS)]
 
     def load(src, dst, sem, j, h):
@@ -86,17 +93,48 @@
             stg.at[j], w.at[j, :, yh, x, at, :], d2_s.at[j], d2_r.at[j], partner
         )
 
-    def yo_copy(j):
-        ref = w.at[j, :, yh, x]
-        return remote(ref, ref, yo_s.at[j], yo_r.at[j], across)
-
-    def x_copy(j, k):
-        ref = w.at[j, :, :, x]
-        return remote(ref, ref, x_s.at[j, k], x_r.at[j, k], (up, down)[k])
-
-    def f_copy(j, k):
-        ref = w.at[j, :, :, (x_dn, x_up)[k], pl.ds(k * rows, rows), :]
-        return remote(ref, ref, f_s.at[j, k], f_r.at[j, k], (up, down)[k])
+    def part_x():
+        return pl.ds(0, PART_X)
+
+    def part_y(h):
+        size = PART_Y // 2
+        return pl.ds(pl.multiple_of(PART_X + h * size, 16), size)
+
+    def part_z():
+        size = PART_Z // ZS
+        return pl.ds(pl.multiple_of(PART_X + PART_Y + z * size, 16), size)
+
+    def yo_copy(j, i):
+        ref = w.at[j, :, yh, x, (part_x(), part_y(1 - yl), part_z())[i], :]
+        return remote(ref, ref, yo_s.at[j, i], yo_r.at[j, i], across)
+
+    def x_copy(j, i, k):
+        ref = w.at[j, :, :, x, (part_x(), part_y(yl), part_z())[i], :]
+        return remote(ref, ref, x_s.at[j, i, k], x_r.at[j, i, k], (up, down)[k])
+
+    def f_copy(j, i, k):
+        ref = w.at[
+            j, k, :, (x_dn, x_up)[k], (part_x(), part_y(yl), part_z())[i], :
+        ]
+        return remote(ref, ref, f_s.at[j, i, k], f_r.at[j, i, k], (up, down)[k])
+
+    def block(j, b, at):
+        if b == 0:
+            return w.at[j, :, 1 - yh, x, at, :]
+        return w.at[j, :, :, (x_up, x_dn, x_far)[b - 1], at, :]
+
+    def yi_copy(j, b):
+        ref = block(j, b, part_y(yl))
+        return remote(ref, ref, yi_s.at[j, b], yi_r.at[j, b], beside)
+
+    def z_copy(j, b, k):
+        ref = block(j, b, part_z())
+        return remote(ref, ref, z_s.at[j, b, k], z_r.at[j, b, k], layers[k])
+
+    def share(j, b):
+        yi_copy(j, b).start()
+        for k in range(3):
+            z_copy(j, b, k).start()
 
     def nt_copy():
         ref = nt.at[pl.ds(pl.multiple_of(core * tokens, tokens), tokens), :]
@@ -213,7 +251,7 @@
 
     nt_copy().start()
 
-    @pl.loop(0, n + 5)
+    @pl.loop(0, n + 6)
     def _(t):
         def stage(lag, fn):
             j = t - lag
@@ -223,13 +261,17 @@
                 fn(j)
 
         def stage_x(j):
-            yo_copy(j).wait_recv()
-            for k in range(2):
-                x_copy(j, k).start()
+            for i in range(3):
+                yo_copy(j, i).wait_recv()
+            for i in range(3):
+                for k in range(2):
+                    x_copy(j, i, k).start()
+            share(j, 0)
 
         def stage_y(j):
             d2_copy(j).wait_recv()
-            yo_copy(j).start()
+            for i in range(3):
+                yo_copy(j, i).start()
 
         def stage_send_sums(j):
             for k in range(GROUPS - 1):
@@ -237,12 +279,25 @@
 
         def stage_forward(j):
             for k in range(2):
-                x_copy(j, k).wait_recv()
-                f_copy(j, k).start()
+                for i in range(3):
+                    x_copy(j, i, k).wait_recv()
+            for i in range(3):
+                for k in range(2):
+                    f_copy(j, i, k).start()
+            share(j, 1)
+            share(j, 2)
+
+        def stage_far(j):
+            for k in range(2):
+                for i in range(3):
+                    f_copy(j, i, k).wait_recv()
+            share(j, 3)
 
         def stage_project(j):
-            for k in range(2):
-                f_copy(j, k).wait_recv()
+            for b in range(4):
+                yi_copy(j, b).wait_recv()
+                for k in range(3):
+                    z_copy(j, b, k).wait_recv()
 
             @pl.when(j == 0)
             def _():
@@ -260,7 +315,8 @@
         stage(-2, scatter)
         stage(0, stage_send_sums)
         stage(4, stage_forward)
-        stage(5, stage_project)
+        stage(5, stage_far)
+        stage(6, stage_project)
 
     nt_copy().wait_send()
 
@@ -270,10 +326,15 @@
             rs_copy(j, k).wait_send()
             sm_copy(j, k).wait_send()
         d2_copy(j).wait_send()
-        yo_copy(j).wait_send()
-        for k in range(2):
-            x_copy(j, k).wait_send()
-            f_copy(j, k).wait_send()
+        for i in range(3):
+            yo_copy(j, i).wait_send()
+            for k in range(2):
+                x_copy(j, i, k).wait_send()
+                f_copy(j, i, k).wait_send()
+        for b in range(4):
+            yi_copy(j, b).wait_send()
+            for k in range(3):
+                z_copy(j, b, k).wait_send()
         both(lambda h: sums_out(j, h).wait())
         own_out(j).wait()
         far_out(j).wait_send()
@@ -312,8 +373,9 @@
             dma((n, GROUPS - 1)), dma((n, GROUPS - 1)),
             dma((n, GROUPS - 1)), dma((n, GROUPS - 1)),
             dma((n,)), dma((n,)), dma((1,)), dma((1,)),
-            dma((n,)), dma((n,)),
-            dma((n, 2)), dma((n, 2)), dma((n, 2)), dma((n, 2)),
+            dma((n, 3)), dma((n, 3)),
+            dma((n, 3, 2)), dma((n, 3, 2)), dma((n, 3, 2)), dma((n, 3, 2)),
+            dma((n, 4)), dma((n, 4)), dma((n, 4, 3)), dma((n, 4, 3)),
             dma((n,)), dma((n,)), dma((n,)), dma((n, 2)),
         ],
         compiler_params=pltpu.CompilerParams(

time: 189 us -> 147 us (0.78)
  Pallas kernels: 177 us -> 134 us
    pallas_call x1, Pallas kernels: 177 us -> 134 us  [fused(): pl.pallas_call(kernel, out_shape=(jax.ShapeDtypeStruct((2, rows, cols), b...]
where the time goes in v2:
time: 147 us; the launch traced here: 146 us
  Pallas kernels  134 us (91%)
  other arithmetic  9.47 us (6%)
  local copies, waits for them, and re-layouts  2.02 us (1%)
    pallas_call x1, Pallas kernels, fused(): pl.pallas_call(kernel, out_shape=(jax.ShapeDtypeStruct((2, rows, cols), b...  134 us
    sub x1, other arithmetic, body(): new_params = outer_params - RATE * (outer_grad + MU * new_momentum)  9.47 us

profile of v2, /device:TPU:1, one launch (start us, length us, event | category | flops | bytes accessed | tf_op | source)
XLA Modules:
  0.0 146.4 jit_solution(14493686632240455567)
XLA Ops:
  0.6 134.3 %shard_map.76 = (bf16[2,128,4096]{2,1,0:T(8,128)(2,1)}, bf16[512,4096]{1,0:T(8,128)(2,1)}) custom-call(bf16[512,2048]{1,0:T(8,128)(2,1)} %tok_ref.1, f32[1,2048]{1,0:T(1,128)} %bitcast.3, f32[2,128,4096]{2,1,0:T(8,128)} %p_ref.1, f32[2,128,4096]{2,1,0:T(8,128)} %m_ref.1, bf16[2,128,4096]{2,1,0:T(8,128)(2,1)} %bitcast.2), custom_call_target="tpu_custom_call" | custom-call | flops 17179869184 | bytes 33554432 | tf_op jit(solution)/shard_map/pallas_call | solution.py:353
  134.9 0.0 copy-start
  134.9 9.5 %multiply_subtract_fusion = (f32[2,128,4096]{2,1,0:T(8,128)}, f32[2,128,4096]{2,1,0:T(8,128)}) fusion(f32[2,128,4096]{2,1,0:T(8,128)} %p_ref.1, bf16[2,128,4096]{2,1,0:T(8,128)(2,1)} %get-tuple-element.5, f32[2,128,4096]{2,1,0:T(8,128)} %m_ref.1), kind=kLoop, calls=%fused_computation | loop fusion | flops 8388608 | bytes 18874368 | tf_op jit(solution)/shard_map/sub | solution.py:396
  144.4 0.0 copy-done
  144.4 2.0 %copy.9 = bf16[512,4096]{1,0:T(8,128)(2,1)} copy(bf16[512,4096]{1,0:T(8,128)(2,1)S(1)} %copy-done) | data formatting | bytes 8388608
Async XLA Ops:
  134.9 9.5 %copy-start = (bf16[512,4096]{1,0:T(8,128)(2,1)S(1)}, bf16[512,4096]{1,0:T(8,128)(2,1)}, u32[]{:S(2)}) copy-start(bf16[512,4096]{1,0:T(8,128)(2,1)} %get-tuple-element.14) | copy-start | bytes 12582916

commit v3 on v2

--- a/solution.py
+++ b/solution.py
@@ -17,9 +17,11 @@
 GROUPS = 8
 XS = 4
 ZS = 4
-PART_X = 96
-PART_Y = 96
+PART_X = 64
+PART_D = 64
+PART_Y = 64
 PART_Z = 64
+NORM_STEPS = 4
 
 
 def kernel(
@@ -28,7 +30,8 @@
     dl, rs, sm, pb, mb, w, stg, tk, nt, ob,
     ld_d, ld_p, ld_m, ld_t,
     rs_s, rs_r, sm_s, sm_r, d2_s, d2_r, nt_s, nt_r,
-    yo_s, yo_r, x_s, x_r, f_s, f_r, yi_s, yi_r, z_s, z_r, o_l, o_s, o_r, so_s,
+    yo_s, yo_r, x_s, x_r, f_s, f_r, yi_s, yi_r, z_s, z_r,
+    xd_s, xd_r, fd_s, fd_r, ac_s, ac_r, o_l, o_s, o_r, so_s,
 ):
     n = CHUNKS
     rows = dl.shape[3]
@@ -96,21 +99,39 @@
     def part_x():
         return pl.ds(0, PART_X)
 
+    def part_d():
+        return pl.ds(PART_X, PART_D)
+
+    def part_xd():
+        return pl.ds(0, PART_X + PART_D)
+
     def part_y(h):
         size = PART_Y // 2
-        return pl.ds(pl.multiple_of(PART_X + h * size, 16), size)
+        return pl.ds(pl.multiple_of(PART_X + PART_D + h * size, 16), size)
 
     def part_z():
         size = PART_Z // ZS
-        return pl.ds(pl.multiple_of(PART_X + PART_Y + z * size, 16), size)
+        return pl.ds(pl.multiple_of(PART_X + PART_D + PART_Y + z * size, 16), size)
 
     def yo_copy(j, i):
-        ref = w.at[j, :, yh, x, (part_x(), part_y(1 - yl), part_z())[i], :]
+        ref = w.at[j, :, yh, x, (part_xd(), part_y(1 - yl), part_z())[i], :]
         return remote(ref, ref, yo_s.at[j, i], yo_r.at[j, i], across)
 
     def x_copy(j, i, k):
         ref = w.at[j, :, :, x, (part_x(), part_y(yl), part_z())[i], :]
         return remote(ref, ref, x_s.at[j, i, k], x_r.at[j, i, k], (up, down)[k])
+
+    def xd_copy(j, k):
+        ref = w.at[j, :, yh, x, part_d(), :]
+        return remote(ref, ref, xd_s.at[j, k], xd_r.at[j, k], (up, down)[k])
+
+    def fd_copy(j, k):
+        ref = w.at[j, k, yh, (x_dn, x_up)[k], part_d(), :]
+        return remote(ref, ref, fd_s.at[j, k], fd_r.at[j, k], (up, down)[k])
+
+    def ac_copy(j, b):
+        ref = w.at[j, :, yh, (x_up, x_dn, x_far)[b - 1], part_d(), :]
+        return remote(ref, ref, ac_s.at[j, b - 1], ac_r.at[j, b - 1], across)
 
     def f_copy(j, i, k):
         ref = w.at[
@@ -135,6 +156,8 @@
         yi_copy(j, b).start()
         for k in range(3):
             z_copy(j, b, k).start()
+        if b > 0:
+            ac_copy(j, b).start()
 
     def nt_copy():
         ref = nt.at[pl.ds(pl.multiple_of(core * tokens, tokens), tokens), :]
@@ -170,13 +193,6 @@
     def _(j):
         both(lambda h: load(d_ref, dl, ld_d, j, h).start())
 
-    pltpu.make_async_copy(tok_ref, tk, ld_t.at[0]).start()
-
-    @pl.loop(0, n)
-    def _(j):
-        both(lambda h: load(p_ref, pb, ld_p, j, h).start())
-        both(lambda h: load(m_ref, mb, ld_m, j, h).start())
-
     barrier = pltpu.get_barrier_semaphore()
     friends = peers + [partner, across, up, down]
     for friend in friends:
@@ -191,17 +207,29 @@
     for j in range(2):
         scatter(j)
 
-    pltpu.make_async_copy(tok_ref, tk, ld_t.at[0]).wait()
-    step = 32
-
-    @pl.loop(0, tokens // step)
-    def _(i):
-        at = pl.multiple_of(i * step, step)
-        values = tk[pl.ds(at, step), :].astype(jnp.float32)
-        mean = jnp.sum(values * values, axis=1, keepdims=True) * (1.0 / width)
-        scaled = values * lax.rsqrt(mean + EPS) * gain_ref[...]
-        base = pl.multiple_of(core * tokens + at, step)
-        nt[pl.ds(base, step), :] = scaled.astype(jnp.bfloat16)
+    pltpu.make_async_copy(tok_ref, tk, ld_t.at[0]).start()
+
+    @pl.loop(0, n)
+    def _(j):
+        both(lambda h: load(p_ref, pb, ld_p, j, h).start())
+        both(lambda h: load(m_ref, mb, ld_m, j, h).start())
+
+    step = 16
+    share_of = tokens // NORM_STEPS
+
+    def norm(part):
+        @pl.when(part == 0)
+        def _():
+            pltpu.make_async_copy(tok_ref, tk, ld_t.at[0]).wait()
+
+        @pl.loop(0, share_of // step)
+        def _(i):
+            at = pl.multiple_of(part * share_of + i * step, step)
+            values = tk[pl.ds(at, step), :].astype(jnp.float32)
+            mean = jnp.sum(values * values, axis=1, keepdims=True) * (1.0 / width)
+            scaled = values * lax.rsqrt(mean + EPS) * gain_ref[...]
+            base = pl.multiple_of(core * tokens + at, step)
+            nt[pl.ds(base, step), :] = scaled.astype(jnp.bfloat16)
 
     def add_up(j):
         for k in range(GROUPS - 1):
@@ -249,8 +277,6 @@
             ) * factor
             ob[j, at, :] = (gate / (1.0 + jnp.exp(-gate)) * raised).astype(jnp.bfloat16)
 
-    nt_copy().start()
-
     @pl.loop(0, n + 6)
     def _(t):
         def stage(lag, fn):
@@ -272,6 +298,8 @@
             d2_copy(j).wait_recv()
             for i in range(3):
                 yo_copy(j, i).start()
+            for k in range(2):
+                xd_copy(j, k).start()
 
         def stage_send_sums(j):
             for k in range(GROUPS - 1):
@@ -279,16 +307,19 @@
 
         def stage_forward(j):
             for k in range(2):
+                xd_copy(j, k).wait_recv()
                 for i in range(3):
                     x_copy(j, i, k).wait_recv()
-            for i in range(3):
-                for k in range(2):
+            for k in range(2):
+                fd_copy(j, k).start()
+                for i in range(3):
                     f_copy(j, i, k).start()
             share(j, 1)
             share(j, 2)
 
         def stage_far(j):
             for k in range(2):
+                fd_copy(j, k).wait_recv()
                 for i in range(3):
                     f_copy(j, i, k).wait_recv()
             share(j, 3)
@@ -298,6 +329,8 @@
                 yi_copy(j, b).wait_recv()
                 for k in range(3):
                     z_copy(j, b, k).wait_recv()
+                if b > 0:
+                    ac_copy(j, b).wait_recv()
 
             @pl.when(j == 0)
             def _():
@@ -314,7 +347,16 @@
         stage(1, lambda j: d2_copy(j).start())
         stage(-2, scatter)
         stage(0, stage_send_sums)
+        @pl.when(t < NORM_STEPS)
+        def _():
+            norm(t)
+
         stage(4, stage_forward)
+
+        @pl.when(t == NORM_STEPS)
+        def _():
+            nt_copy().start()
+
         stage(5, stage_far)
         stage(6, stage_project)
 
@@ -335,6 +377,11 @@
             yi_copy(j, b).wait_send()
             for k in range(3):
                 z_copy(j, b, k).wait_send()
+            if b > 0:
+                ac_copy(j, b).wait_send()
+        for k in range(2):
+            xd_copy(j, k).wait_send()
+            fd_copy(j, k).wait_send()
         both(lambda h: sums_out(j, h).wait())
         own_out(j).wait()
         far_out(j).wait_send()
@@ -376,6 +423,7 @@
             dma((n, 3)), dma((n, 3)),
             dma((n, 3, 2)), dma((n, 3, 2)), dma((n, 3, 2)), dma((n, 3, 2)),
             dma((n, 4)), dma((n, 4)), dma((n, 4, 3)), dma((n, 4, 3)),
+            dma((n, 2)), dma((n, 2)), dma((n, 2)), dma((n, 2)), dma((n, 3)), dma((n, 3)),
             dma((n,)), dma((n,)), dma((n,)), dma((n, 2)),
         ],
         compiler_params=pltpu.CompilerParams(

time: 147 us -> 139 us (0.946)
  Pallas kernels: 134 us -> 126 us
    pallas_call x1, Pallas kernels: 134 us -> 126 us  [fused(): pl.pallas_call(kernel, out_shape=(jax.ShapeDtypeStruct((2, rows, cols), b...]
where the time goes in v3:
time: 139 us; the launch traced here: 138 us
  Pallas kernels  126 us (91%)
  other arithmetic  9.47 us (7%)
  local copies, waits for them, and re-layouts  2.02 us (1%)
    pallas_call x1, Pallas kernels, fused(): pl.pallas_call(kernel, out_shape=(jax.ShapeDtypeStruct((2, rows, cols), b...  126 us
    sub x1, other arithmetic, body(): new_params = outer_params - RATE * (outer_grad + MU * new_momentum)  9.47 us

profile of v3, /device:TPU:1, one launch (start us, length us, event | category | flops | bytes accessed | tf_op | source)
XLA Modules:
  0.0 138.4 jit_solution(622616078940904595)
XLA Ops:
  0.6 126.2 %shard_map.76 = (bf16[2,128,4096]{2,1,0:T(8,128)(2,1)}, bf16[512,4096]{1,0:T(8,128)(2,1)}) custom-call(bf16[512,2048]{1,0:T(8,128)(2,1)} %tok_ref.1, f32[1,2048]{1,0:T(1,128)} %bitcast.3, f32[2,128,4096]{2,1,0:T(8,128)} %p_ref.1, f32[2,128,4096]{2,1,0:T(8,128)} %m_ref.1, bf16[2,128,4096]{2,1,0:T(8,128)(2,1)} %bitcast.2), custom_call_target="tpu_custom_call" | custom-call | flops 17179869184 | bytes 33554432 | tf_op jit(solution)/shard_map/pallas_call | solution.py:400
  126.9 0.0 copy-start
  126.9 9.5 %multiply_subtract_fusion = (f32[2,128,4096]{2,1,0:T(8,128)}, f32[2,128,4096]{2,1,0:T(8,128)}) fusion(f32[2,128,4096]{2,1,0:T(8,128)} %p_ref.1, bf16[2,128,4096]{2,1,0:T(8,128)(2,1)} %get-tuple-element.5, f32[2,128,4096]{2,1,0:T(8,128)} %m_ref.1), kind=kLoop, calls=%fused_computation | loop fusion | flops 8388608 | bytes 18874368 | tf_op jit(solution)/shard_map/sub | solution.py:444
  136.4 0.0 copy-done
  136.4 2.0 %copy.9 = bf16[512,4096]{1,0:T(8,128)(2,1)} copy(bf16[512,4096]{1,0:T(8,128)(2,1)S(1)} %copy-done) | data formatting | bytes 8388608
Async XLA Ops:
  126.9 9.5 %copy-start = (bf16[512,4096]{1,0:T(8,128)(2,1)S(1)}, bf16[512,4096]{1,0:T(8,128)(2,1)}, u32[]{:S(2)}) copy-start(bf16[512,4096]{1,0:T(8,128)(2,1)} %get-tuple-element.14) | copy-start | bytes 12582916

commit v4 on v0

v4 whole, which is shorter than its diff:
```python
import functools
import math

import jax
import jax.numpy as jnp
from jax import lax
from jax.experimental import pallas as pl
from jax.experimental.pallas import tpu as pltpu
from jax.sharding import PartitionSpec as P

EPS = 1e-05
MU = 0.9
RATE = 0.7
MESH = pl.DeviceIdType.MESH

CHUNKS = 16
WIDE = CHUNKS // 2
GROUPS = 8
XS = 4
ZS = 4
NORM_STEPS = 4
WAYS = "DYZX"
LAG_Y, LAG_X, LAG_F, LAG_FAR, LAG_P = 4, 6, 9, 12, 15


def kernel(
    tok_ref, gain_ref, p_ref, m_ref, d_ref,
    np_ref, nm_ref, hid_ref,
    dl, rs, sm, w, stg, tk, nt, ob,
    ld_d, ld_p, ld_m, ld_t,
    rs_s, rs_r, sm_s, sm_r, d2_s, d2_r, nt_s, nt_r,
    yo_s, yo_r, x_s, x_r, f_s, f_r, sh_s, sh_r, o_s, o_r,
):
    n = CHUNKS
    rows = dl.shape[3]
    wide = dl.shape[4]
    wc = w.shape[5]
    half = n * wc
    piece = rows // GROUPS
    tokens = tk.shape[0]
    width = tk.shape[1]

    rep = lax.axis_index("rep")
    fs = lax.axis_index("fsdp")
    core = lax.rem(fs, 2)
    other = 1 - core
    chip = fs // 2
    x = lax.rem(chip, XS)
    yh = chip // XS
    yl = lax.rem(rep, 2)
    z = rep // 2
    x_up = lax.rem(x + 1, XS)
    x_dn = lax.rem(x + XS - 1, XS)
    x_far = lax.rem(x + 2, XS)

    def fsdp_of(yh_, x_, core_):
        return (yh_ * XS + x_) * 2 + core_

    partner = (rep, fsdp_of(yh, x, other))
    across = (z * 2 + 1 - yl, fsdp_of(1 - yh, x, core))
    up = (rep, fsdp_of(yh, x_up, core))
    down = (rep, fsdp_of(yh, x_dn, core))
    beside = (z * 2 + 1 - yl, fs)
    layers = [(lax.rem(z + k, ZS) * 2 + yl, fs) for k in (1, 2, 3)]
    peers = [(lax.rem(rep + k, GROUPS), fs) for k in range(1, GROUPS)]

    def wide_columns(jj, h):
        return pl.ds(pl.multiple_of(h * half + jj * wide, wide), wide)

    def load(src, dst, sem, jj, h):
        return pltpu.make_async_copy(
            src.at[:, :, wide_columns(jj, h)], dst.at[jj, h], sem.at[jj, h]
        )

    def load_state(src, dst, sem, jj, h):
        at = wide_columns(jj, h)
        return pltpu.make_async_copy(
            src.at[:, :, at], dst.at[:, :, at], sem.at[jj, h]
        )

    def remote(src, dst, send, recv, device):
        return pltpu.make_async_remote_copy(
            src_ref=src, dst_ref=dst, send_sem=send, recv_sem=recv,
            device_id=device, device_id_type=MESH,
        )

    def rs_copy(jj, k):
        rows_of = pl.multiple_of(peers[k][0] * piece, piece)
        return remote(
            dl.at[jj, :, :, pl.ds(rows_of, piece), :], rs.at[jj, k],
            rs_s.at[jj, k], rs_r.at[jj, k], peers[k],
        )

    def sm_copy(jj, k):
        mine = pl.ds(pl.multiple_of(rep * piece, piece), piece)
        ref = sm.at[jj, :, :, mine, :]
        return remote(ref, ref, sm_s.at[jj, k], sm_r.at[jj, k], peers[k])

    def d2_copy(jj):
        at = pl.ds(pl.multiple_of(core * rows, rows), rows)
        pair = pl.ds(2 * jj, 2)
        return remote(
            stg.at[pair], w.at[pair, :, yh, x, at, :], d2_s.at[jj], d2_r.at[jj], partner
        )

    def rows_all():
        return pl.ds(0, 2 * rows)

    def rows_half(h):
        return pl.ds(pl.multiple_of(h * rows, rows), rows)

    def rows_quarter():
        size = 2 * rows // ZS
        return pl.ds(pl.multiple_of(z * size, size), size)

    def part(way):
        if way == "Y":
            return rows_half(yl)
        if way == "Z":
            return rows_quarter()
        return rows_all()

    def yo_copy(way, j):
        at = rows_half(1 - yl) if way == "Y" else part(way)
        ref = w.at[j, :, yh, x, at, :]
        return remote(ref, ref, yo_s.at[j], yo_r.at[j], across)

    def x_copy(way, j, k):
        if way == "D":
            ref = w.at[j, :, yh, x]
        else:
            ref = w.at[j, :, :, x, part(way), :]
        return remote(ref, ref, x_s.at[j, k], x_r.at[j, k], (up, down)[k])

    def f_copy(way, j, k):
        from_x = (x_dn, x_up)[k]
        if way == "D":
            ref = w.at[j, k, yh, from_x]
        else:
            ref = w.at[j, k, :, from_x, part(way), :]
        return remote(ref, ref, f_s.at[j, k], f_r.at[j, k], (up, down)[k])

    def last_legs(way, j, b):
        from_x = (x, x_up, x_dn, x_far)[b]
        if way == "X":
            return []
        if way == "D":
            if b == 0:
                return [yo_copy(way, j)]
            ref = w.at[j, :, yh, from_x]
            return [remote(ref, ref, sh_s.at[j, b, 0], sh_r.at[j, b, 0], across)]
        if b == 0:
            ref = w.at[j, :, 1 - yh, x, part(way), :]
        else:
            ref = w.at[j, :, :, from_x, part(way), :]
        targets = [beside] if way == "Y" else layers
        return [
            remote(ref, ref, sh_s.at[j, b, k], sh_r.at[j, b, k], target)
            for k, target in enumerate(targets)
        ]

    def share(way, j, b):
        for copy in last_legs(way, j, b):
            copy.start()

    def nt_copy():
        ref = nt.at[pl.ds(pl.multiple_of(core * tokens, tokens), tokens), :]
        return remote(ref, ref, nt_s.at[0], nt_r.at[0], partner)

    def column(j):
        return pl.ds(pl.multiple_of(core * half + j * wc, wc), wc)

    def far_out(j):
        return remote(
            ob.at[j], hid_ref.at[:, column(j)], o_s.at[j], o_r.at[j], partner
        )

    def both(fn):
        for h in range(2):
            fn(h)

    @pl.loop(0, WIDE)
    def _(jj):
        both(lambda h: load(d_ref, dl, ld_d, jj, h).start())

    barrier = pltpu.get_barrier_semaphore()
    friends = peers + [partner, across, up, down]
    for friend in friends:
        pl.semaphore_signal(barrier, inc=1, device_id=friend, device_id_type=MESH)
    pl.semaphore_wait(barrier, len(friends))

    def scatter(jj):
        both(lambda h: load(d_ref, dl, ld_d, jj, h).wait())
        for k in range(GROUPS - 1):
            rs_copy(jj, k).start()

    for jj in range(2):
        scatter(jj)

    pltpu.make_async_copy(tok_ref, tk, ld_t.at[0]).start()

    @pl.loop(0, WIDE)
    def _(jj):
        both(lambda h: load_state(p_ref, np_ref, ld_p, jj, h).start())
        both(lambda h: load_state(m_ref, nm_ref, ld_m, jj, h).start())

    step = 16
    share_of = tokens // NORM_STEPS

    def norm(index):
        if index == 0:
            pltpu.make_async_copy(tok_ref, tk, ld_t.at[0]).wait()

        @pl.loop(0, share_of // step)
        def _(i):
            at = pl.multiple_of(index * share_of + i * step, step)
            values = tk[pl.ds(at, step), :].astype(jnp.float32)
            mean = jnp.sum(values * values, axis=1, keepdims=True) * (1.0 / width)
            scaled = values * lax.rsqrt(mean + EPS) * gain_ref[...]
            base = pl.multiple_of(core * tokens + at, step)
            nt[pl.ds(base, step), :] = scaled.astype(jnp.bfloat16)

    def add_up(jj):
        for k in range(GROUPS - 1):
            rs_copy(jj, k).wait_recv()
        mine = pl.ds(pl.multiple_of(rep * piece, piece), piece)
        for h in range(2):
            for q in range(2):
                total = dl[jj, h, q, mine, :].astype(jnp.float32)
                for k in range(GROUPS - 1):
                    total = total + rs[jj, k, h, q].astype(jnp.float32)
                sm[jj, h, q, mine, :] = total.astype(jnp.bfloat16)

    def send_sums(jj):
        for k in range(GROUPS - 1):
            sm_copy(jj, k).start()

    def update(jj):
        for k in range(GROUPS - 1):
            sm_copy(jj, k).wait_recv()
        both(lambda h: load_state(p_ref, np_ref, ld_p, jj, h).wait())
        both(lambda h: load_state(m_ref, nm_ref, ld_m, jj, h).wait())
        at = pl.ds(pl.multiple_of(core * rows, rows), rows)

        def weights(h, q):
            grad = sm[jj, h, q].astype(jnp.float32) * (1.0 / GROUPS)
            cols = wide_columns(jj, h)
            moment = MU * nm_ref[q, :, cols] + grad
            fresh = np_ref[q, :, cols] - RATE * (grad + MU * moment)
            nm_ref[q, :, cols] = moment
            np_ref[q, :, cols] = fresh
            return fresh.astype(jnp.bfloat16)

        for q in range(2):
            fresh = weights(other, q)
            for i in range(2):
                stg[2 * jj + i, q] = fresh[:, i * wc:(i + 1) * wc]
        for q in range(2):
            fresh = weights(core, q)
            for i in range(2):
                w[2 * jj + i, q, yh, x, at, :] = fresh[:, i * wc:(i + 1) * wc]

    def hand_over(jj):
        d2_copy(jj).start()

    factor = 1.0 / math.sqrt(width)
    tile = 256

    def project(j):
        def piece_of(base, i):
            left = nt[pl.ds(pl.multiple_of(base * tokens + i * tile, tile), tile), :]
            right = jnp.concatenate(
                [w[j, 0].reshape(width, wc), w[j, 1].reshape(width, wc)], axis=1
            )
            sums = jnp.dot(left, right, preferred_element_type=jnp.float32) * factor
            gate, raised = sums[:, :wc], sums[:, wc:]
            return (gate / (1.0 + jnp.exp(-gate)) * raised).astype(jnp.bfloat16)

        @pl.loop(0, tokens // tile)
        def _(i):
            at = pl.ds(pl.multiple_of(i * tile, tile), tile)
            ob[j, at, :] = piece_of(other, i)

        far_out(j).start()

        @pl.loop(0, tokens // tile)
        def _(i):
            at = pl.ds(pl.multiple_of(i * tile, tile), tile)
            hid_ref[at, column(j)] = piece_of(core, i)

    def stage_y(way, j, first):
        if first:
            d2_copy(j // 2).wait_recv()
        yo_copy(way, j).start()
        if way == "D":
            for k in range(2):
                x_copy(way, j, k).start()

    def stage_x(way, j):
        if way == "D":
            return
        yo_copy(way, j).wait_recv()
        for k in range(2):
            x_copy(way, j, k).start()
        share(way, j, 0)

    def stage_forward(way, j):
        for k in range(2):
            x_copy(way, j, k).wait_recv()
        for k in range(2):
            f_copy(way, j, k).start()
        share(way, j, 1)
        share(way, j, 2)

    def stage_far(way, j):
        for k in range(2):
            f_copy(way, j, k).wait_recv()
        share(way, j, 3)

    def stage_project(way, j):
        for b in range(4):
            for copy in last_legs(way, j, b):
                copy.wait_recv()
        project(j)

    cycle = len(WAYS)
    turns = -(-(n + LAG_P) // cycle)

    @pl.loop(0, turns)
    def _(turn):
        for slot in range(cycle):
            t = turn * cycle + slot

            def stage(lag, fn):
                j = t - lag
                way = WAYS[(slot - lag) % cycle]

                @pl.when(jnp.logical_and(j >= 0, j < n))
                def _():
                    fn(way, j)

            def wide_stage(ahead, fn):
                jj = t // 2 + ahead

                @pl.when(jnp.logical_and(jj >= 0, jj < WIDE))
                def _():
                    fn(jj)

            stage(LAG_X, stage_x)
            stage(LAG_Y, lambda way, j: stage_y(way, j, (slot - LAG_Y) % 2 == 0))
            if slot % 2 == 1:
                wide_stage(-1, update)
            else:
                wide_stage(0, add_up)
                wide_stage(0, send_sums)
                wide_stage(2, scatter)
            for index in range(NORM_STEPS):
                if index % cycle == slot:

                    @pl.when(t == index)
                    def _():
                        norm(index)

            if NORM_STEPS % cycle == slot:

                @pl.when(t == NORM_STEPS)
                def _():
                    nt_copy().start()

            if slot % 2 == 1:
                wide_stage(-1, hand_over)
            stage(LAG_F, stage_forward)
            stage(LAG_FAR, stage_far)
            if LAG_P % cycle == slot:

                @pl.when(t == LAG_P)
                def _():
                    nt_copy().wait_recv()

            stage(LAG_P, stage_project)

    nt_copy().wait_send()

    @pl.loop(0, WIDE)
    def _(jj):
        for k in range(GROUPS - 1):
            rs_copy(jj, k).wait_send()
            sm_copy(jj, k).wait_send()
        d2_copy(jj).wait_send()

    @pl.loop(0, n // cycle)
    def _(turn):
        for slot, way in enumerate(WAYS):
            j = turn * cycle + slot
            if way != "D":
                yo_copy(way, j).wait_send()
            for k in range(2):
                x_copy(way, j, k).wait_send()
                f_copy(way, j, k).wait_send()
            for b in range(4):
                for copy in last_legs(way, j, b):
                    copy.wait_send()
            far_out(j).wait_send()
            far_out(j).wait_recv()


def fused(tokens, gain, params, moment, deltas):
    count, width = tokens.shape
    _, rows, cols = params.shape
    n = CHUNKS
    wc = cols // (2 * n)
    wide = 2 * wc
    piece = rows // GROUPS
    bf16, f32 = jnp.bfloat16, jnp.float32
    dma = pltpu.SemaphoreType.DMA
    any_spec = pl.BlockSpec(memory_space=pl.ANY)
    return pl.pallas_call(
        kernel,
        out_shape=(
            pltpu.VMEM((2, rows, cols), f32),
            pltpu.VMEM((2, rows, cols), f32),
            pltpu.VMEM((count, cols), bf16),
        ),
        in_specs=[any_spec, pl.BlockSpec(memory_space=pltpu.VMEM), any_spec, any_spec, any_spec],
        out_specs=(pl.BlockSpec(memory_space=pltpu.VMEM),) * 3,
        scratch_shapes=[
            pltpu.VMEM((WIDE, 2, 2, rows, wide), bf16),
            pltpu.VMEM((WIDE, GROUPS - 1, 2, 2, piece, wide), bf16),
            pltpu.VMEM((WIDE, 2, 2, rows, wide), bf16),
            pltpu.VMEM((n, 2, 2, XS, 2 * rows, wc), bf16),
            pltpu.VMEM((n, 2, rows, wc), bf16),
            pltpu.VMEM((count, width), bf16),
            pltpu.VMEM((2 * count, width), bf16),
            pltpu.VMEM((n, count, wc), bf16),
            dma((WIDE, 2)), dma((WIDE, 2)), dma((WIDE, 2)), dma((1,)),
            dma((WIDE, GROUPS - 1)), dma((WIDE, GROUPS - 1)),
            dma((WIDE, GROUPS - 1)), dma((WIDE, GROUPS - 1)),
            dma((WIDE,)), dma((WIDE,)), dma((1,)), dma((1,)),
            dma((n,)), dma((n,)),
            dma((n, 2)), dma((n, 2)), dma((n, 2)), dma((n, 2)),
            dma((n, 4, 3)), dma((n, 4, 3)),
            dma((n,)), dma((n,)),
        ],
        compiler_params=pltpu.CompilerParams(
            collective_id=0, has_side_effects=True, vmem_limit_bytes=50 * 2**20
        ),
        cost_estimate=pl.CostEstimate(
            flops=4 * count * width * cols, bytes_accessed=2**25, transcendentals=count * cols
        ),
    )(tokens, gain, params, moment, deltas)


def body(tokens, norm_gain, outer_params, momentum, deltas):
    return fused(tokens, norm_gain.reshape(1, -1), outer_params, momentum, deltas[0])


def solution(mesh):
    in_specs = (
        P(("rep", "fsdp"), None),
        P(),
        P(None, "fsdp", None),
        P(None, "fsdp", None),
        P("rep", None, "fsdp", None),
    )
    out_specs = (P(None, "fsdp", None), P(None, "fsdp", None), P(("rep", "fsdp"), None))
    return jax.shard_map(body, mesh=mesh, in_specs=in_specs, out_specs=out_specs, check_vma=False)
```

time: 376 us -> 130 us (0.35)
  waiting for transfers between devices: 316 us -> 0 us
  Pallas kernels: 0 us -> 123 us
  matrix products: 34.9 us -> 0 us
  between operations: 13.7 us -> 0.64 us
  other arithmetic: 9.89 us -> 0 us
  local copies, waits for them, and re-layouts: 1.59 us -> 6.04 us
    all_gather x2 -> x0, waiting for transfers between devices: 205 us -> none  [body(): lax.all_gather(weights[which], 'fsdp', axis=0, tiled=True)]
    pallas_call x0 -> x1, Pallas kernels: none -> 123 us  [fused(): pl.pallas_call(kernel, out_shape=(pltpu.VMEM((2, rows, cols), f32), pltpu...]
    psum x1 -> x0, waiting for transfers between devices: 110 us -> none  [body(): summed = lax.psum(own_delta.astype(jnp.bfloat16), 'rep').astype(jnp.float32)]
    dot_general x2 -> x0, matrix products: 34.9 us -> none  [body(): jnp.dot(normed, lax.all_gather(weights[which], 'fsdp', axis=0, tiled=True...]
    convert_element_type x1 -> x0, other arithmetic: 9.4 us -> none  [body(): weights = new_params.astype(jnp.bfloat16)]
    unnamed x4 -> x3, local copies, waits for them, and re-layouts: 0.13 us -> 6.04 us
  transfers between devices with their start and end apart: 3 -> 0, of which waited for: 3 -> 0; matrix products, arithmetic and copies ran while one was open for 4% -> 0% of each run, Pallas kernels for 0% -> 0%
where the time goes in v4:
time: 130 us; the launch traced here: 129 us
  Pallas kernels  123 us (95%)
  local copies, waits for them, and re-layouts  6.04 us (5%)
    pallas_call x1, Pallas kernels, fused(): pl.pallas_call(kernel, out_shape=(pltpu.VMEM((2, rows, cols), f32), pltpu...  123 us
    unnamed x3, local copies, waits for them, and re-layouts  6.04 us

profile of v4, /device:TPU:1, one launch (start us, length us, event | category | flops | bytes accessed | tf_op | source)
XLA Modules:
  0.0 129.4 jit_solution(5210679139131720041)
XLA Ops:
  0.6 122.7 %shard_map.76 = (f32[2,128,4096]{2,1,0:T(8,128)S(1)}, f32[2,128,4096]{2,1,0:T(8,128)S(1)}, bf16[512,4096]{1,0:T(8,128)(2,1)S(1)}) custom-call(bf16[512,2048]{1,0:T(8,128)(2,1)} %tok_ref.1, f32[1,2048]{1,0:T(1,128)} %bitcast.3, f32[2,128,4096]{2,1,0:T(8,128)} %p_ref.1, f32[2,128,4096]{2,1,0:T(8,128)} %m_ref.1, bf16[2,128,4096]{2,1,0:T(8,128)(2,1)} %bitcast.2), custom_call_target="tpu_custom_call" | custom-call | flops 17179869184 | bytes 33554432 | tf_op jit(solution)/shard_map/pallas_call | solution.py:417
  123.3 2.0 %copy.11 = f32[2,128,4096]{2,1,0:T(8,128)} copy(f32[2,128,4096]{2,1,0:T(8,128)S(1)} %get-tuple-element.3) | data formatting | bytes 8388608
  125.4 2.0 %copy.12 = f32[2,128,4096]{2,1,0:T(8,128)} copy(f32[2,128,4096]{2,1,0:T(8,128)S(1)} %get-tuple-element.4) | data formatting | bytes 8388608
  127.4 2.0 %copy.13 = bf16[512,4096]{1,0:T(8,128)(2,1)} copy(bf16[512,4096]{1,0:T(8,128)(2,1)S(1)} %get-tuple-element.5) | data formatting | bytes 8388608

commit v5 on v4

--- a/solution.py
+++ b/solution.py
@@ -20,7 +20,7 @@
 ZS = 4
 NORM_STEPS = 4
 WAYS = "DYZX"
-LAG_Y, LAG_X, LAG_F, LAG_FAR, LAG_P = 4, 6, 9, 12, 15
+LAG_Y, LAG_X, LAG_F, LAG_FAR, LAG_P = 4, 6, 8, 10, 12
 
 
 def kernel(
@@ -88,13 +88,13 @@
         rows_of = pl.multiple_of(peers[k][0] * piece, piece)
         return remote(
             dl.at[jj, :, :, pl.ds(rows_of, piece), :], rs.at[jj, k],
-            rs_s.at[jj, k], rs_r.at[jj, k], peers[k],
+            rs_s.at[jj], rs_r.at[jj], peers[k],
         )
 
     def sm_copy(jj, k):
         mine = pl.ds(pl.multiple_of(rep * piece, piece), piece)
         ref = sm.at[jj, :, :, mine, :]
-        return remote(ref, ref, sm_s.at[jj, k], sm_r.at[jj, k], peers[k])
+        return remote(ref, ref, sm_s.at[jj], sm_r.at[jj], peers[k])
 
     def d2_copy(jj):
         at = pl.ds(pl.multiple_of(core * rows, rows), rows)
@@ -130,7 +130,7 @@
             ref = w.at[j, :, yh, x]
         else:
             ref = w.at[j, :, :, x, part(way), :]
-        return remote(ref, ref, x_s.at[j, k], x_r.at[j, k], (up, down)[k])
+        return remote(ref, ref, x_s.at[j], x_r.at[j], (up, down)[k])
 
     def f_copy(way, j, k):
         from_x = (x_dn, x_up)[k]
@@ -138,7 +138,7 @@
             ref = w.at[j, k, yh, from_x]
         else:
             ref = w.at[j, k, :, from_x, part(way), :]
-        return remote(ref, ref, f_s.at[j, k], f_r.at[j, k], (up, down)[k])
+        return remote(ref, ref, f_s.at[j], f_r.at[j], (up, down)[k])
 
     def last_legs(way, j, b):
         from_x = (x, x_up, x_dn, x_far)[b]
@@ -148,16 +148,45 @@
             if b == 0:
                 return [yo_copy(way, j)]
             ref = w.at[j, :, yh, from_x]
-            return [remote(ref, ref, sh_s.at[j, b, 0], sh_r.at[j, b, 0], across)]
+            return [remote(ref, ref, sh_s.at[j, b], sh_r.at[j, b], across)]
         if b == 0:
             ref = w.at[j, :, 1 - yh, x, part(way), :]
         else:
             ref = w.at[j, :, :, from_x, part(way), :]
         targets = [beside] if way == "Y" else layers
         return [
-            remote(ref, ref, sh_s.at[j, b, k], sh_r.at[j, b, k], target)
+            remote(ref, ref, sh_s.at[j, b], sh_r.at[j, b], target)
             for k, target in enumerate(targets)
         ]
+
+    def rs_all(jj):
+        return remote(rs.at[jj], rs.at[jj], rs_s.at[jj], rs_r.at[jj], partner)
+
+    def sm_all(jj):
+        return remote(rs.at[jj], rs.at[jj], sm_s.at[jj], sm_r.at[jj], partner)
+
+    def x_all(way, j):
+        if way == "D":
+            ref = w.at[j, :, 0, pl.ds(0, 2)]
+        else:
+            ref = w.at[j, :, :, pl.ds(0, 2), part(way), :]
+        return remote(ref, ref, x_s.at[j], x_r.at[j], partner)
+
+    def f_all(way, j):
+        if way == "D":
+            ref = w.at[j, 0, 0, pl.ds(0, 2)]
+        else:
+            ref = w.at[j, 0, :, pl.ds(0, 2), part(way), :]
+        return remote(ref, ref, f_s.at[j], f_r.at[j], partner)
+
+    def last_all(way, j, b):
+        if way != "Z":
+            return last_legs(way, j, b)
+        if b == 0:
+            ref = w.at[j, :, 0, pl.ds(0, 3), part(way), :]
+        else:
+            ref = w.at[j, :, :, pl.ds(0, 3), part(way), :]
+        return [remote(ref, ref, sh_s.at[j, b], sh_r.at[j, b], partner)]
 
     def share(way, j, b):
         for copy in last_legs(way, j, b):
@@ -221,8 +250,7 @@
             nt[pl.ds(base, step), :] = scaled.astype(jnp.bfloat16)
 
     def add_up(jj):
-        for k in range(GROUPS - 1):
-            rs_copy(jj, k).wait_recv()
+        rs_all(jj).wait_recv()
         mine = pl.ds(pl.multiple_of(rep * piece, piece), piece)
         for h in range(2):
             for q in range(2):
@@ -236,8 +264,7 @@
             sm_copy(jj, k).start()
 
     def update(jj):
-        for k in range(GROUPS - 1):
-            sm_copy(jj, k).wait_recv()
+        sm_all(jj).wait_recv()
         both(lambda h: load_state(p_ref, np_ref, ld_p, jj, h).wait())
         both(lambda h: load_state(m_ref, nm_ref, ld_m, jj, h).wait())
         at = pl.ds(pl.multiple_of(core * rows, rows), rows)
@@ -305,21 +332,19 @@
         share(way, j, 0)
 
     def stage_forward(way, j):
-        for k in range(2):
-            x_copy(way, j, k).wait_recv()
+        x_all(way, j).wait_recv()
         for k in range(2):
             f_copy(way, j, k).start()
         share(way, j, 1)
         share(way, j, 2)
 
     def stage_far(way, j):
-        for k in range(2):
-            f_copy(way, j, k).wait_recv()
+        f_all(way, j).wait_recv()
         share(way, j, 3)
 
     def stage_project(way, j):
         for b in range(4):
-            for copy in last_legs(way, j, b):
+            for copy in last_all(way, j, b):
                 copy.wait_recv()
         project(j)
 
@@ -383,9 +408,8 @@
 
     @pl.loop(0, WIDE)
     def _(jj):
-        for k in range(GROUPS - 1):
-            rs_copy(jj, k).wait_send()
-            sm_copy(jj, k).wait_send()
+        rs_all(jj).wait_send()
+        sm_all(jj).wait_send()
         d2_copy(jj).wait_send()
 
     @pl.loop(0, n // cycle)
@@ -394,11 +418,10 @@
             j = turn * cycle + slot
             if way != "D":
                 yo_copy(way, j).wait_send()
-            for k in range(2):
-                x_copy(way, j, k).wait_send()
-                f_copy(way, j, k).wait_send()
+            x_all(way, j).wait_send()
+            f_all(way, j).wait_send()
             for b in range(4):
-                for copy in last_legs(way, j, b):
+                for copy in last_all(way, j, b):
                     copy.wait_send()
             far_out(j).wait_send()
             far_out(j).wait_recv()
@@ -433,12 +456,11 @@
             pltpu.VMEM((2 * count, width), bf16),
             pltpu.VMEM((n, count, wc), bf16),
             dma((WIDE, 2)), dma((WIDE, 2)), dma((WIDE, 2)), dma((1,)),
-            dma((WIDE, GROUPS - 1)), dma((WIDE, GROUPS - 1)),
-            dma((WIDE, GROUPS - 1)), dma((WIDE, GROUPS - 1)),
+            dma((WIDE,)), dma((WIDE,)), dma((WIDE,)), dma((WIDE,)),
             dma((WIDE,)), dma((WIDE,)), dma((1,)), dma((1,)),
             dma((n,)), dma((n,)),
-            dma((n, 2)), dma((n, 2)), dma((n, 2)), dma((n, 2)),
-            dma((n, 4, 3)), dma((n, 4, 3)),
+            dma((n,)), dma((n,)), dma((n,)), dma((n,)),
+            dma((n, 4)), dma((n, 4)),
             dma((n,)), dma((n,)),
         ],
         compiler_params=pltpu.CompilerParams(

time: 130 us -> 124 us (0.954)
  Pallas kernels: 123 us -> 117 us
    pallas_call x1, Pallas kernels: 123 us -> 117 us  [fused(): pl.pallas_call(kernel, out_shape=(pltpu.VMEM((2, rows, cols), f32), pltpu...]
where the time goes in v5:
time: 124 us; the launch traced here: 123 us
  Pallas kernels  117 us (94%)
  local copies, waits for them, and re-layouts  6.04 us (5%)
    pallas_call x1, Pallas kernels, fused(): pl.pallas_call(kernel, out_shape=(pltpu.VMEM((2, rows, cols), f32), pltpu...  117 us
    unnamed x3, local copies, waits for them, and re-layouts  6.04 us

profile of v5, /device:TPU:1, one launch (start us, length us, event | category | flops | bytes accessed | tf_op | source)
XLA Modules:
  0.0 123.4 jit_solution(11235888237591871427)
XLA Ops:
  0.6 116.7 %shard_map.76 = (f32[2,128,4096]{2,1,0:T(8,128)S(1)}, f32[2,128,4096]{2,1,0:T(8,128)S(1)}, bf16[512,4096]{1,0:T(8,128)(2,1)S(1)}) custom-call(bf16[512,2048]{1,0:T(8,128)(2,1)} %tok_ref.1, f32[1,2048]{1,0:T(1,128)} %bitcast.3, f32[2,128,4096]{2,1,0:T(8,128)} %p_ref.1, f32[2,128,4096]{2,1,0:T(8,128)} %m_ref.1, bf16[2,128,4096]{2,1,0:T(8,128)(2,1)} %bitcast.2), custom_call_target="tpu_custom_call" | custom-call | flops 17179869184 | bytes 33554432 | tf_op jit(solution)/shard_map/pallas_call | solution.py:440
  117.4 2.0 %copy.11 = f32[2,128,4096]{2,1,0:T(8,128)} copy(f32[2,128,4096]{2,1,0:T(8,128)S(1)} %get-tuple-element.3) | data formatting | bytes 8388608
  119.4 2.0 %copy.12 = f32[2,128,4096]{2,1,0:T(8,128)} copy(f32[2,128,4096]{2,1,0:T(8,128)S(1)} %get-tuple-element.4) | data formatting | bytes 8388608
  121.4 2.0 %copy.13 = bf16[512,4096]{1,0:T(8,128)(2,1)} copy(bf16[512,4096]{1,0:T(8,128)(2,1)S(1)} %get-tuple-element.5) | data formatting | bytes 8388608

commit v6 on v5

--- a/solution.py
+++ b/solution.py
@@ -373,6 +373,8 @@
 
             stage(LAG_X, stage_x)
             stage(LAG_Y, lambda way, j: stage_y(way, j, (slot - LAG_Y) % 2 == 0))
+            stage(LAG_F, stage_forward)
+            stage(LAG_FAR, stage_far)
             if slot % 2 == 1:
                 wide_stage(-1, update)
             else:
@@ -394,8 +396,6 @@
 
             if slot % 2 == 1:
                 wide_stage(-1, hand_over)
-            stage(LAG_F, stage_forward)
-            stage(LAG_FAR, stage_far)
             if LAG_P % cycle == slot:
 
                 @pl.when(t == LAG_P)

time: 124 us -> 124 us (level)
  no operation moved by 1% of the time
where the time goes in v6:
time: 124 us
  Pallas kernels  117 us (94%)
  local copies, waits for them, and re-layouts  6.04 us (5%)
    pallas_call x1, Pallas kernels, fused(): pl.pallas_call(kernel, out_shape=(pltpu.VMEM((2, rows, cols), f32), pltpu...  117 us
    unnamed x3, local copies, waits for them, and re-layouts  6.04 us

profile of v6, /device:TPU:1, one launch (start us, length us, event | category | flops | bytes accessed | tf_op | source)
XLA Modules:
  0.0 123.5 jit_solution(8894691725038365196)
XLA Ops:
  0.6 116.9 %shard_map.76 = (f32[2,128,4096]{2,1,0:T(8,128)S(1)}, f32[2,128,4096]{2,1,0:T(8,128)S(1)}, bf16[512,4096]{1,0:T(8,128)(2,1)S(1)}) custom-call(bf16[512,2048]{1,0:T(8,128)(2,1)} %tok_ref.1, f32[1,2048]{1,0:T(1,128)} %bitcast.3, f32[2,128,4096]{2,1,0:T(8,128)} %p_ref.1, f32[2,128,4096]{2,1,0:T(8,128)} %m_ref.1, bf16[2,128,4096]{2,1,0:T(8,128)(2,1)} %bitcast.2), custom_call_target="tpu_custom_call" | custom-call | flops 17179869184 | bytes 33554432 | tf_op jit(solution)/shard_map/pallas_call | solution.py:440
  117.5 2.0 %copy.11 = f32[2,128,4096]{2,1,0:T(8,128)} copy(f32[2,128,4096]{2,1,0:T(8,128)S(1)} %get-tuple-element.3) | data formatting | bytes 8388608
  119.5 2.0 %copy.12 = f32[2,128,4096]{2,1,0:T(8,128)} copy(f32[2,128,4096]{2,1,0:T(8,128)S(1)} %get-tuple-element.4) | data formatting | bytes 8388608
  121.5 2.0 %copy.13 = bf16[512,4096]{1,0:T(8,128)(2,1)} copy(bf16[512,4096]{1,0:T(8,128)(2,1)S(1)} %get-tuple-element.5) | data formatting | bytes 8388608
